TPU v7x, 32 devices: a 4x2x2 block of a 4x4x8 slice. The times are simulated.
32 devices in a mesh: data: 4 (over y, z), seq: 8 (over x, core).
Axes of the slice: x: 4, y: 2, z: 2, core: 2. Of those that a mesh axis runs over, the one named last changes fastest.
The devices are a block of a 4x4x8 slice.
Arguments:
- tokens: bfloat16 [32, 256, 384], P('data', 'seq'), parts along dimension 0
- lengths: int32 [32], P('data'), parts along dimension 0
- slot_param: bfloat16 [384, 512], replicated
- logit_scale: float32 [], replicated
- w_in: bfloat16 [256, 384, 1536], P('seq')
- w_out: bfloat16 [256, 1536, 384], P('seq')
Outputs:
- output: bfloat16 [32, 256, 384], P('data', 'seq'), parts along dimension 0
There are 4 independent parts. A program takes and returns all parts, laid end to end along the dimension named above; an argument that names none is the same for every part.
All inputs are finite; a program needn't handle non-finite values.
Results may differ from a plain program's by a relative error of at most 0.0171172.
Values are sent between devices in bfloat16 or wider.
A program may use at most 768 MiB of HBM per device.

v0:
```python
import jax
import jax.numpy as jnp
from jax import lax
from jax.sharding import PartitionSpec as P

EPSILON = 1e-6
NEG_FILL = -1e30


def l2_normed(values, axis_dim):
    v32 = values.astype(jnp.float32)
    return (v32 * lax.rsqrt(jnp.sum(v32 * v32, axis=axis_dim, keepdims=True) + EPSILON)).astype(jnp.bfloat16)


def solution(mesh):
    seq_size = mesh.shape["seq"]

    def local_layer(tok_blk, len_blk, slot_param, logit_scale, w_in, w_out):
        batch_loc, tok_loc, d_model = tok_blk.shape
        n_slots = slot_param.shape[1]
        exp_loc = w_in.shape[0]
        slot_loc = n_slots // seq_size
        per_exp = slot_loc // exp_loc
        positions = lax.axis_index("seq") * tok_loc + jnp.arange(tok_loc, dtype=jnp.int32)
        tok_valid = (positions[None, :] < len_blk[:, None])[:, :, None]
        logits = logit_scale * jnp.einsum("btd,dn->btn", l2_normed(tok_blk, 2), l2_normed(slot_param, 0), preferred_element_type=jnp.float32)
        masked = jnp.where(tok_valid, logits, NEG_FILL)
        col_max = lax.pmax(jnp.max(masked, axis=1, keepdims=True), "seq")
        disp_w = jnp.exp(masked - col_max)
        col_sum = lax.psum_scatter(jnp.sum(disp_w, axis=1), "seq", scatter_dimension=1, tiled=True)
        part_sum = jnp.einsum("btn,btd->bnd", disp_w.astype(jnp.bfloat16), tok_blk, preferred_element_type=jnp.float32)
        slot_sum = lax.psum_scatter(part_sum.astype(jnp.bfloat16), "seq", scatter_dimension=1, tiled=True)
        slot_in = (slot_sum.astype(jnp.float32) / col_sum[:, :, None]).astype(jnp.bfloat16)
        slot_grp = slot_in.reshape(batch_loc, exp_loc, per_exp, d_model)
        hidden = jax.nn.gelu(jnp.einsum("besd,edf->besf", slot_grp, w_in, preferred_element_type=jnp.float32)).astype(jnp.bfloat16)
        own_out = jnp.einsum("besf,efd->besd", hidden, w_out, preferred_element_type=jnp.float32).astype(jnp.bfloat16)
        slot_out = lax.all_gather(own_out.reshape(batch_loc, slot_loc, d_model), "seq", axis=1, tiled=True)
        comb_w = jnp.exp(logits - jnp.max(logits, axis=2, keepdims=True))
        row_sum = jnp.sum(comb_w, axis=2, keepdims=True)
        tok_mixed = jnp.einsum("btn,bnd->btd", comb_w.astype(jnp.bfloat16), slot_out, preferred_element_type=jnp.float32) / row_sum
        return jnp.where(tok_valid, tok_mixed, 0.0).astype(jnp.bfloat16)

    return jax.shard_map(local_layer, mesh=mesh, in_specs=(P("data", "seq", None), P("data"), P(None, None), P(), P("seq", None, None), P("seq", None, None)), out_specs=P("data", "seq", None), check_vma=False)
```

profile of v0, /device:TPU:81, one launch (start us, length us, event | category | flops | bytes accessed | tf_op | source)
XLA Modules:
  0.0 164.4 jit_solution(11382366639815329884)
XLA Ops:
  6.5 0.0 copy-start
  6.5 0.0 reduce-scatter.7.cloned.1.call-start
  7.3 1.1 fusion.30
  8.4 1.0 fusion.36
  9.4 0.7 broadcast_compare_fusion
  10.2 1.6 fusion.54
  11.7 24.0 %pmax.7 = f32[8,512]{1,0:T(8,128)S(1)} all-reduce(f32[8,512]{1,0:T(8,128)S(1)} %get-tuple-element.8), channel_id=1, replica_groups=mesh['data'=4,'seq'=8] {'seq'}, use_global_device_ids=true, to_apply=%region_4.5 | all-reduce | flops 4096 | bytes 32768 | tf_op jit(solution)/shard_map/pmax | solution.py:28
  35.7 0.3 fusion.32
  36.0 0.8 copy.14
  36.8 0.1 reduce-scatter.7.cloned.1.call-update
  36.9 0.1 reduce-scatter.5.cloned.1.call-start
  37.0 0.0 copy-done
  37.0 3.0 %convolution_convert_fusion = bf16[8,512,384]{2,1,0:T(8,128)(2,1)} fusion(bf16[8,32,384]{2,1,0:T(8,128)(2,1)S(1)} %copy-done, f32[8,32,512]{2,1,0:T(8,128)S(1)} %get-tuple-element.9, f32[8,512]{1,0:T(8,128)S(1)} %pmax.7, pred[8,32]{1,0:T(8,128)(4,1)S(1)} %broadcast_compare_fusion), kind=kOutput, calls=%fused_computation.14 | convolution fusion | flops 102629376 | bytes 3883264 | tf_op jit(solution)/shard_map/btn,btd->bnd/dot_general | solution.py:31
  40.0 0.1 reduce-scatter.5.cloned.1.call-update
  40.1 0.1 all-gather.2.cloned.1.call-start
  40.1 25.5 %reduce-scatter.7.cloned.1.call-done = f32[64,8]{1,0:T(8,128)} async-done(((f32[512,8]{1,0:T(8,128)}), f32[64,8]{1,0:T(8,128)}) %reduce-scatter.7.cloned.1.call-update) | async-done | bytes 2064
  65.6 0.8 copy.15
  66.5 32.7 %reduce-scatter.5.cloned.1.call-done = bf16[8,64,384]{2,1,0:T(8,128)(2,1)} async-done(((bf16[8,512,384]{2,1,0:T(8,128)(2,1)}), bf16[8,64,384]{2,1,0:T(8,128)(2,1)}) %reduce-scatter.5.cloned.1.call-update) | async-done | bytes 393232 | tf_op jit(solution)/shard_map/reduce_scatter | solution.py:32
  99.2 1.1 divide_convert_fusion
  100.4 0.2 copy.13
  100.6 26.3 %fusion.23 = bf16[32,8,2,384]{3,1,2,0:T(8,128)(2,1)S(1)} fusion(bf16[32,1536,384]{2,1,0:T(8,128)(2,1)} %param.11, bf16[8,32,2,384]{3,0,2,1:T(8,128)(2,1)S(1)} %bitcast.42, bf16[32,384,1536]{2,1,0:T(8,128)(2,1)} %param.10), kind=kOutput, calls=%fused_computation.19 | convolution fusion | flops 1215234048 | bytes 76283904 | tf_op jit(solution)/shard_map/besf,efd->besd/dot_general | solution.py:36
  126.9 0.8 copy.10
  127.7 0.1 all-gather.2.cloned.1.call-update
  127.7 26.9 %all-gather.2.cloned.1.call-done = bf16[8,512,384]{2,1,0:T(8,128)(2,1)} async-done(((bf16[8,64,384]{2,1,0:T(8,128)(2,1)}), bf16[8,512,384]{2,1,0:T(8,128)(2,1)}) %all-gather.2.cloned.1.call-update) | async-done | bytes 3145744 | tf_op jit(solution)/shard_map/all_gather | solution.py:37
  154.7 3.2 %fusion.29 = bf16[8,32,384]{2,1,0:T(8,128)(2,1)} fusion(bf16[8,512,384]{2,1,0:T(8,128)(2,1)} %all-gather.2.cloned.1.call-done, f32[8,32,512]{2,1,0:T(8,128)S(1)} %get-tuple-element.9, f32[8,32]{1,0:T(8,128)S(1)} %get-tuple-element.7, f32[8,32]{1,0:T(8,128)S(1)} %get-tuple-element.5, pred[8,32]{1,0:T(8,128)(4,1)S(1)} %broadcast_compare_fusion), kind=kOutput, calls=%fused_computation.23 | convolution fusion | flops 101220352 | bytes 3868928 | tf_op jit(solution)/shard_map/btn,bnd->btd/dot_general | solution.py:40
  (3 shorter events, 0.0 us)
Async XLA Ops:
  6.5 30.4 %copy-start = (bf16[8,32,384]{2,1,0:T(8,128)(2,1)S(1)}, bf16[8,32,384]{2,1,0:T(8,128)(2,1)}, u32[]{:S(2)}) copy-start(bf16[8,32,384]{2,1,0:T(8,128)(2,1)} %param.6) | copy-start | bytes 589828
  6.5 59.1 %reduce-scatter.7.cloned.1.call-start = ((), (), s32[]{:S(2)}) async-start(), calls=%async_computation.4 | async-start | bytes 294912
  36.9 62.3 %reduce-scatter.5.cloned.1.call-start = ((), (), s32[]{:S(2)}) async-start(), calls=%async_computation.2 | async-start | bytes 3538944 | tf_op jit(solution)/shard_map/reduce_scatter | solution.py:32
  40.1 114.6 %all-gather.2.cloned.1.call-start = ((), (), s32[]{:S(2)}) async-start(), calls=%async_computation.3 | async-start | bytes 3538944 | tf_op jit(solution)/shard_map/all_gather | solution.py:37
Sparse Core Ops, SparseCore 0:
  37.0 28.5 reduce-scatter.6
  68.0 31.1 reduce-scatter.4
  127.9 26.7 all-gather.1
where the time goes:
time: 165 us; the launch traced here: 164 us
  waiting for transfers between devices  85.3 us (52%)
  matrix products  34 us (21%)
  blocking collectives  24 us (15%)
  between operations  13.9 us (8%)
  other arithmetic  4.32 us (3%)
  local copies, waits for them, and re-layouts  2.67 us (2%)
    reduce_scatter x1, waiting for transfers between devices, local_layer(): lax.psum_scatter(part_sum.astype(jnp.bfloat16), 'seq', scatter_dimension=...  32.7 us
    all_gather x1, waiting for transfers between devices, local_layer(): lax.all_gather(own_out.reshape(batch_loc, slot_loc, d_model), 'seq', axis...  26.9 us
    dot_general x1, matrix products, local_layer(): jnp.einsum('besf,efd->besd', hidden, w_out, preferred_element_type=jnp.fl...  26.3 us
    unnamed x4, waiting for transfers between devices  25.7 us
    pmax x1, blocking collectives, local_layer(): col_max = lax.pmax(jnp.max(masked, axis=1, keepdims=True), 'seq')  24 us
  transfers between devices with their start and end apart: 3, of which 3 were waited for; matrix products, arithmetic and copies ran while one was open for 2% of the time, Pallas kernels for 0%

commit v1 on v0

v1 whole, which is shorter than its diff:
```python
import functools

import jax
import jax.numpy as jnp
from jax import lax
from jax.experimental import pallas as pl
from jax.experimental.pallas import tpu as pltpu
from jax.sharding import PartitionSpec as P

EPSILON = 1e-6
NEG_FILL = -1e30
F32 = jnp.float32
BF16 = jnp.bfloat16
LANES = 128

OWN_R, OWN_L, OWN_P, FWD_R, FWD_L, L_TO_P, R_TO_P, FR_TO_P, FL_TO_P = range(9)
KINDS = 9

W_SLOTS = 22
CHUNK = 4
SEQ_CHUNK = 2
LAG1 = 4
LAG2 = 7


def unit(values, axis):
    v = values.astype(F32)
    return v * lax.rsqrt(jnp.sum(v * v, axis=axis, keepdims=True) + EPSILON)


def kernel(n_dev, tok, lens, phi, gain, w_in, w_out, out,
           xg, yg, w1, w2, xs, pnt, cexp, hid, rowinv,
           sem1, sem2, tsend, trecv, ysend, yrecv):
    n_seq, n_tok, d_model = tok.shape
    n_exp = w_in.shape[0]
    n_slot = phi.shape[1]
    per_dev = n_slot // n_dev
    per_exp = per_dev // n_exp
    rows = n_seq * per_exp
    n_chunk = n_exp // CHUNK
    n_tchunk = n_seq // SEQ_CHUNK
    n_chip = n_dev // 2
    all_tok = n_dev * n_tok
    own_tok = n_seq * n_tok

    me = lax.axis_index("seq")
    chip, core = me // 2, lax.rem(me, 2)
    right = lax.rem(chip + 1, n_chip) * 2 + core
    left = lax.rem(chip + n_chip - 1, n_chip) * 2 + core
    far = lax.rem(chip + 2, n_chip) * 2 + core
    partner = chip * 2 + 1 - core
    g = gain[0]

    def w1_copy(e, slot):
        return pltpu.make_async_copy(w_in.at[e], w1.at[slot], sem1.at[slot])

    def w2_copy(e, slot):
        return pltpu.make_async_copy(w_out.at[e], w2.at[slot], sem2.at[slot])

    for e in range(W_SLOTS):
        w1_copy(e, e).start()
        w2_copy(e, e).start()

    barrier = pltpu.get_barrier_semaphore()
    for peer in (right, left, partner):
        pl.semaphore_signal(barrier, inc=1, device_id={"seq": peer}, device_id_type=pl.DeviceIdType.MESH)
    pl.semaphore_wait(barrier, 3)

    dest = {OWN_R: right, OWN_L: left, FWD_R: right, FWD_L: left}
    half = SEQ_CHUNK // 2
    ehalf = CHUNK // 2

    def tcopy(kind, k):
        origin = {OWN_R: me, OWN_L: me, OWN_P: me, FWD_R: left, FWD_L: right, L_TO_P: left, R_TO_P: right, FR_TO_P: far, FL_TO_P: far}[kind]
        lo, num = k * SEQ_CHUNK, SEQ_CHUNK
        if kind in (FWD_R, FR_TO_P):
            num = half
        if kind in (FWD_L, FL_TO_P):
            lo, num = lo + half, half
        dst = xg.at[pl.ds(lo, num), origin]
        src = tok.at[pl.ds(lo, num)] if kind in (OWN_R, OWN_L, OWN_P) else dst
        return pltpu.make_async_remote_copy(src_ref=src, dst_ref=dst, send_sem=tsend.at[kind, k], recv_sem=trecv.at[kind, k],
                                            device_id={"seq": dest.get(kind, partner)}, device_id_type=pl.DeviceIdType.MESH)

    def ycopy(kind, k):
        origin = {OWN_R: me, OWN_L: me, OWN_P: me, FWD_R: left, FWD_L: right, L_TO_P: left, R_TO_P: right, FR_TO_P: far, FL_TO_P: far}[kind]
        lo, num = 0, CHUNK
        if kind in (FWD_R, FR_TO_P):
            num = ehalf
        if kind in (FWD_L, FL_TO_P):
            lo, num = ehalf, ehalf
        ref = yg.at[k, origin, pl.ds(lo, num)]
        return pltpu.make_async_remote_copy(src_ref=ref, dst_ref=ref, send_sem=ysend.at[kind, k], recv_sem=yrecv.at[kind, k],
                                            device_id={"seq": dest.get(kind, partner)}, device_id_type=pl.DeviceIdType.MESH)

    def send_own(copy, k):
        for kind in (OWN_R, OWN_L, OWN_P):
            copy(kind, k).start()

    def relay_near(copy, k):
        copy(OWN_R, k).wait_recv()
        copy(FWD_R, k).start()
        copy(L_TO_P, k).start()
        copy(OWN_L, k).wait_recv()
        copy(FWD_L, k).start()
        copy(R_TO_P, k).start()

    def relay_far(copy, k):
        copy(FWD_R, k).wait_recv()
        copy(FR_TO_P, k).start()
        copy(FWD_L, k).wait_recv()
        copy(FL_TO_P, k).start()

    def wait_partner(copy, k):
        for kind in (OWN_P, L_TO_P, R_TO_P, FR_TO_P, FL_TO_P):
            copy(kind, k).wait_recv()

    def wait_sends(copy, k):
        for kind in range(KINDS):
            copy(kind, k).wait_send()

    for k in range(n_tchunk):
        send_own(tcopy, k)

    for b in range(n_seq):
        xg[b, me] = tok[b]

    pn32 = unit(phi[...], 0)
    pn = pn32.astype(BF16)
    slabs = d_model // LANES
    pnt32 = pn.astype(F32).T
    for j in range(slabs):
        pnt[j] = pnt32[:, j * LANES:(j + 1) * LANES]

    def strided_rows(ref, start, size, stride):
        return jnp.concatenate([ref[j, pl.ds(start, size, stride=stride), :] for j in range(slabs)], axis=1)

    own_rows = jnp.concatenate([strided_rows(pnt, me * per_dev + s, n_exp, per_exp) for s in range(per_exp)], axis=0).astype(BF16)

    relay_near(tcopy, 0)

    own = tok[...].reshape(own_tok, d_model)
    own_unit = unit(own, 1).astype(BF16)
    logits = g * jnp.dot(own_unit, pn, preferred_element_type=F32)
    comb = jnp.exp(logits - jnp.max(logits, axis=1, keepdims=True))
    rowinv[...] = 1.0 / jnp.sum(comb, axis=1, keepdims=True)
    comb = comb.astype(BF16)

    relay_near(tcopy, 1)
    relay_far(tcopy, 0)

    width = 256
    devs = width // (CHUNK * rows)
    src = lax.broadcasted_iota(jnp.int32, (devs * per_dev, width), 0)
    col = lax.broadcasted_iota(jnp.int32, (devs * per_dev, width), 1)
    base = col // (CHUNK * rows) * per_dev + lax.rem(col, CHUNK * rows) // rows * per_exp + lax.rem(col, per_exp)
    row_seq = lax.broadcasted_iota(jnp.int32, (own_tok, width), 0) // n_tok
    col_seq = lax.rem(lax.broadcasted_iota(jnp.int32, (own_tok, width), 1), rows) // per_exp
    same = row_seq == col_seq

    def spread(k):
        pick = (src == base + k * (CHUNK * per_exp)).astype(F32).astype(BF16)
        for d in range(n_dev // devs):
            part = jnp.dot(comb[:, d * devs * per_dev:(d + 1) * devs * per_dev], pick, preferred_element_type=F32)
            cexp[k, :, d * width:(d + 1) * width] = jnp.where(same, part, 0.0).astype(BF16)

    for k in range(n_chunk // 2):
        spread(k)
    relay_near(tcopy, 2)
    relay_far(tcopy, 1)
    for k in range(n_chunk // 2, n_chunk):
        spread(k)
    relay_near(tcopy, 3)
    relay_far(tcopy, 2)

    pos = lax.broadcasted_iota(jnp.int32, (per_dev, all_tok), 1)

    def dispatch(b):
        x = xg[b].reshape(all_tok, d_model)
        xn = unit(x, 1).astype(BF16)
        lt = g * lax.dot_general(own_rows, xn, (((1,), (1,)), ((), ())), preferred_element_type=F32)
        lt = jnp.where(pos < lens[b], lt, NEG_FILL)
        e = jnp.exp(lt - jnp.max(lt, axis=1, keepdims=True))
        z = jnp.sum(e, axis=1, keepdims=True)
        s = jnp.dot(e.astype(BF16), x, preferred_element_type=F32) / z
        s = s.astype(BF16).astype(F32)
        for j in range(slabs):
            xs[j, b * per_dev:(b + 1) * per_dev, :] = s[:, j * LANES:(j + 1) * LANES]

    for k in range(n_tchunk):
        if k == n_tchunk - 1:
            relay_far(tcopy, k)
        wait_partner(tcopy, k)
        for b in range(k * SEQ_CHUNK, (k + 1) * SEQ_CHUNK):
            dispatch(b)

    def up(e, slot, u):
        x = strided_rows(xs, e, rows, n_exp).astype(BF16)
        hid[u] = jax.nn.gelu(jnp.dot(x, w1[slot], preferred_element_type=F32)).astype(BF16)

    def down(k, e, u):
        slot = lax.rem(e, W_SLOTS)
        yg[k, me, u] = jnp.dot(hid[u], w2[slot], preferred_element_type=F32).astype(BF16)

    for u in range(CHUNK):
        w1_copy(u, u).wait()
    for u in range(CHUNK):
        up(u, u, u)
    for u in range(CHUNK):
        if u + W_SLOTS < n_exp:
            w1_copy(u + W_SLOTS, u).start()

    def comm(k):
        send_own(ycopy, k - 1)

        @pl.when(k >= LAG1)
        def _():
            relay_near(ycopy, k - LAG1)

        @pl.when(k >= LAG2)
        def _():
            relay_far(ycopy, k - LAG2)

    def step(k, carry):
        first = k * CHUNK

        @pl.when(k >= 1)
        def _():
            comm(k)

        last = k == n_chunk - 1
        for u in range(CHUNK):
            e = first + u
            w2_copy(e, lax.rem(e, W_SLOTS)).wait()

            @pl.when(jnp.logical_not(last))
            def _():
                w1_copy(e + CHUNK, lax.rem(e + CHUNK, W_SLOTS)).wait()
        for u in range(CHUNK):
            down(k, first + u, u)
        for u in range(CHUNK):
            e = jnp.minimum(first + CHUNK + u, n_exp - 1)
            up(e, lax.rem(e, W_SLOTS), u)
        for u in range(CHUNK):
            e = first + u

            @pl.when(e + W_SLOTS < n_exp)
            def _():
                w2_copy(e + W_SLOTS, lax.rem(e, W_SLOTS)).start()

            @pl.when(e + CHUNK + W_SLOTS < n_exp)
            def _():
                w1_copy(e + CHUNK + W_SLOTS, lax.rem(e + CHUNK, W_SLOTS)).start()
        return carry

    lax.fori_loop(0, n_chunk, step, 0)

    acc = jnp.zeros((own_tok, d_model), F32)

    def combine(acc, k):
        wait_partner(ycopy, k)
        y = yg[k].reshape(n_dev * CHUNK * rows, d_model)
        return acc + jnp.dot(cexp[k], y, preferred_element_type=F32)

    send_own(ycopy, n_chunk - 1)
    for k in range(n_chunk, n_chunk + LAG2):
        if 0 <= k - LAG1 < n_chunk:
            relay_near(ycopy, k - LAG1)
        if 0 <= k - LAG2 < n_chunk:
            relay_far(ycopy, k - LAG2)
        if 0 <= k - LAG2 - 1 < n_chunk:
            acc = combine(acc, k - LAG2 - 1)
    acc = combine(acc, n_chunk - 1)

    y = (acc * rowinv[...]).reshape(n_seq, n_tok, d_model)
    tpos = lax.broadcasted_iota(jnp.int32, (n_tok, d_model), 0) + me * n_tok
    for b in range(n_seq):
        out[b] = jnp.where(tpos < lens[b], y[b], 0.0).astype(BF16)

    for k in range(n_tchunk):
        wait_sends(tcopy, k)
    for k in range(n_chunk):
        wait_sends(ycopy, k)


def solution(mesh):
    n_dev = mesh.shape["seq"]

    def local_layer(tok_blk, len_blk, slot_param, logit_scale, w_in, w_out):
        n_seq, n_tok, d_model = tok_blk.shape
        n_exp, _, d_ff = w_in.shape
        n_slot = slot_param.shape[1]
        per_exp = n_slot // n_dev // n_exp
        rows = n_seq * per_exp
        n_chunk = n_exp // CHUNK
        vmem = pl.BlockSpec(memory_space=pltpu.VMEM)
        smem = pl.BlockSpec(memory_space=pltpu.SMEM)
        hbm = pl.BlockSpec(memory_space=pl.ANY)
        return pl.pallas_call(
            functools.partial(kernel, n_dev),
            out_shape=jax.ShapeDtypeStruct(tok_blk.shape, BF16),
            in_specs=[vmem, smem, vmem, smem, hbm, hbm],
            out_specs=vmem,
            scratch_shapes=[
                pltpu.VMEM((n_seq, n_dev, n_tok, d_model), BF16),
                pltpu.VMEM((n_chunk, n_dev, CHUNK, rows, d_model), BF16),
                pltpu.VMEM((W_SLOTS, d_model, d_ff), BF16),
                pltpu.VMEM((W_SLOTS, d_ff, d_model), BF16),
                pltpu.VMEM((d_model // LANES, n_slot, LANES), F32),
                pltpu.VMEM((d_model // LANES, n_slot, LANES), F32),
                pltpu.VMEM((n_chunk, n_seq * n_tok, n_dev * CHUNK * rows), BF16),
                pltpu.VMEM((CHUNK, rows, d_ff), BF16),
                pltpu.VMEM((n_seq * n_tok, 1), F32),
                pltpu.SemaphoreType.DMA((W_SLOTS,)),
                pltpu.SemaphoreType.DMA((W_SLOTS,)),
                pltpu.SemaphoreType.DMA((KINDS, n_seq // SEQ_CHUNK)),
                pltpu.SemaphoreType.DMA((KINDS, n_seq // SEQ_CHUNK)),
                pltpu.SemaphoreType.DMA((KINDS, n_chunk)),
                pltpu.SemaphoreType.DMA((KINDS, n_chunk)),
            ],
            compiler_params=pltpu.CompilerParams(collective_id=0, has_side_effects=True, vmem_limit_bytes=67000000),
            name="soft_moe",
        )(tok_blk, len_blk, slot_param, logit_scale.reshape(1), w_in, w_out)

    return jax.shard_map(local_layer, mesh=mesh, in_specs=(P("data", "seq", None), P("data"), P(None, None), P(), P("seq", None, None), P("seq", None, None)), out_specs=P("data", "seq", None), check_vma=False)
```

time: 165 us -> 46.8 us (0.28)
  waiting for transfers between devices: 85.3 us -> 0 us
  Pallas kernels: 0 us -> 44.4 us
  matrix products: 34 us -> 0 us
  blocking collectives: 24 us -> 0 us
  between operations: 13.9 us -> 0.66 us
  other arithmetic: 4.32 us -> 0 us
    pallas_call x0 -> x1, Pallas kernels: none -> 44.4 us  [local_layer(): pl.pallas_call(functools.partial(kernel, n_dev), out_shape=jax.ShapeDtype...]
    dot_general x4 -> x0, matrix products: 34 us -> none  [the longest x1 26.3 us: local_layer(): jnp.einsum('besf,efd->besd', hidden, w_out, preferred_element_type=jnp.fl...]
    reduce_scatter x1 -> x0, waiting for transfers between devices: 32.7 us -> none  [local_layer(): lax.psum_scatter(part_sum.astype(jnp.bfloat16), 'seq', scatter_dimension=...]
    all_gather x1 -> x0, waiting for transfers between devices: 26.9 us -> none  [local_layer(): lax.all_gather(own_out.reshape(batch_loc, slot_loc, d_model), 'seq', axis...]
    unnamed x4 -> x0, waiting for transfers between devices: 25.7 us -> none
    pmax x1 -> x0, blocking collectives: 24 us -> none  [local_layer(): col_max = lax.pmax(jnp.max(masked, axis=1, keepdims=True), 'seq')]
    reduce_sum x3 -> x0, other arithmetic: 2.43 us -> none  [the longest x2 2.15 us: l2_normed(): jnp.sum(v32 * v32, axis=axis_dim, keepdims=True) + EPSILON]
  transfers between devices with their start and end apart: 3 -> 0, of which waited for: 3 -> 0; matrix products, arithmetic and copies ran while one was open for 2% -> 0% of each run, Pallas kernels for 0% -> 0%
where the time goes in v1:
time: 46.8 us; the launch traced here: 46.6 us
  Pallas kernels  44.4 us (95%)
  local copies, waits for them, and re-layouts  1.62 us (3%)
  between operations  0.66 us (1%)
    pallas_call x1, Pallas kernels, local_layer(): pl.pallas_call(functools.partial(kernel, n_dev), out_shape=jax.ShapeDtype...  44.4 us
    unnamed x1, local copies, waits for them, and re-layouts  1.62 us

profile of v1, /device:TPU:81, one launch (start us, length us, event | category | flops | bytes accessed | tf_op | source)
XLA Modules:
  0.0 46.6 jit_solution(17804230128287084444)
XLA Ops:
  0.7 44.4 %soft_moe.1 = bf16[8,32,384]{2,1,0:T(8,128)(2,1)} custom-call(bf16[8,32,384]{2,1,0:T(8,128)(2,1)} %tok.1, s32[8]{0:T(128)} %lens.1, bf16[384,512]{1,0:T(8,128)(2,1)} %phi.1, f32[1]{0:T(128)} %bitcast.1.gain, bf16[32,384,1536]{2,1,0:T(8,128)(2,1)} %w_in.1, bf16[32,1536,384]{2,1,0:T(8,128)(2,1)} %w_out.1), custom_call_target="tpu_custom_call" | custom-call | tf_op jit(solution)/shard_map/soft_moe/pallas_call | solution.py:299
  45.0 1.6 %copy.9 = bf16[8,32,384]{2,1,0:T(8,128)(2,1)} copy(bf16[8,32,384]{2,1,0:T(8,128)(2,1)} %soft_moe.1) | data formatting | bytes 393216

commit v2 on v0

v2 whole, which is shorter than its diff:
```python
import functools

import jax
import jax.numpy as jnp
from jax import lax
from jax.experimental import pallas as pl
from jax.experimental.pallas import tpu as pltpu
from jax.sharding import PartitionSpec as P

EPSILON = 1e-6
NEG_FILL = -1e30
F32 = jnp.float32
BF16 = jnp.bfloat16
LANES = 128
MESH = pl.DeviceIdType.MESH

OWN_R, OWN_L, OWN_P, FWD_R, FWD_L, L_TO_P, R_TO_P, FAR_TO_P = range(8)
UNITS_SENT = 7
UNITS_FROM_PARTNER = 4
FROM_LEFT, FROM_RIGHT, FAR, PARTNER = range(4)
RECV = {OWN_R: FROM_LEFT, OWN_L: FROM_RIGHT, FWD_R: FAR, FWD_L: FAR}

CHUNK = 4
W_SLOTS = 5
SEQ_CHUNK = 2
LAG = 4


def unit(values, axis):
    v = values.astype(F32)
    return v * lax.rsqrt(jnp.sum(v * v, axis=axis, keepdims=True) + EPSILON)


def kernel(n_dev, tok_hbm, lens_hbm, phi_hbm, gain, w_in, w_out, out,
           tok, phi, lens, xg, yg, w1, w2, xs, pnt, cexp, hid, rowinv,
           insem, sem1, sem2, tsend, trecv, ysend, yrecv):
    n_seq, n_tok, d_model = tok.shape
    n_exp = w_in.shape[0]
    n_slot = phi.shape[1]
    per_dev = n_slot // n_dev
    per_exp = per_dev // n_exp
    rows = n_seq * per_exp
    n_chunk = n_exp // CHUNK
    n_tchunk = n_seq // SEQ_CHUNK
    n_chip = n_dev // 2
    all_tok = n_dev * n_tok
    own_tok = n_seq * n_tok
    slabs = d_model // LANES

    me = lax.axis_index("seq")
    chip, core = me // 2, lax.rem(me, 2)
    right = lax.rem(chip + 1, n_chip) * 2 + core
    left = lax.rem(chip + n_chip - 1, n_chip) * 2 + core
    far = lax.rem(chip + 2, n_chip) * 2 + core
    partner = chip * 2 + 1 - core

    barrier = pltpu.get_barrier_semaphore()
    for peer in (right, left, partner):
        pl.semaphore_signal(barrier, inc=1, device_id={"seq": peer}, device_id_type=MESH)

    tok_in = pltpu.make_async_copy(tok_hbm, tok, insem.at[0])
    phi_in = pltpu.make_async_copy(phi_hbm, phi, insem.at[1])
    lens_in = pltpu.make_async_copy(lens_hbm, lens, insem.at[2])
    tok_in.start()
    phi_in.start()
    lens_in.start()

    def w1_copy(k, slot):
        return pltpu.make_async_copy(w_in.at[pl.ds(k * CHUNK, CHUNK)], w1.at[slot], sem1.at[slot])

    def w2_copy(k, slot):
        return pltpu.make_async_copy(w_out.at[pl.ds(k * CHUNK, CHUNK)], w2.at[slot], sem2.at[slot])

    for k in range(W_SLOTS):
        w1_copy(k, k).start(priority=1)
        w2_copy(k, k).start(priority=1)

    dest = {OWN_R: right, OWN_L: left, FWD_R: right, FWD_L: left}
    origins = {FWD_R: left, FWD_L: right, L_TO_P: left, R_TO_P: right, FAR_TO_P: far}

    def part(kind, size):
        if kind == FWD_R:
            return 0, size // 2
        if kind == FWD_L:
            return size // 2, size // 2
        return 0, size

    def remote(src, dst, send_sem, recv_sem, device):
        return pltpu.make_async_remote_copy(src_ref=src, dst_ref=dst, send_sem=send_sem, recv_sem=recv_sem,
                                            device_id={"seq": device}, device_id_type=MESH)

    class Tokens:
        def send(kind, k):
            lo, num = part(kind, SEQ_CHUNK)
            lo = lo + k * SEQ_CHUNK
            dst = xg.at[pl.ds(lo, num), origins.get(kind, me)]
            src = dst if kind in origins else tok.at[pl.ds(lo, num)]
            remote(src, dst, tsend, trecv.at[RECV.get(kind, PARTNER), k], dest.get(kind, partner)).start()

        def arrived(what, k):
            units = UNITS_FROM_PARTNER if what == PARTNER else 1
            ref = xg.at[pl.ds(k * SEQ_CHUNK, SEQ_CHUNK), pl.ds(0, units)]
            remote(ref, ref, tsend, trecv.at[what, k], partner).wait_recv()

        def all_sent():
            ref = xg.at[:, pl.ds(0, UNITS_SENT)]
            remote(ref, ref, tsend, trecv.at[0, 0], partner).wait_send()

    class Slots:
        def send(kind, k):
            lo, num = part(kind, CHUNK)
            ref = yg.at[k, origins.get(kind, me), pl.ds(lo, num)]
            remote(ref, ref, ysend, yrecv.at[RECV.get(kind, PARTNER), k], dest.get(kind, partner)).start()

        def arrived(what, k):
            units = UNITS_FROM_PARTNER if what == PARTNER else 1
            ref = yg.at[k, pl.ds(0, units)]
            remote(ref, ref, ysend, yrecv.at[what, k], partner).wait_recv()

        def all_sent():
            ref = yg.at[:, pl.ds(0, UNITS_SENT)]
            remote(ref, ref, ysend, yrecv.at[0, 0], partner).wait_send()

    def send_own(gather, k):
        for kind in (OWN_R, OWN_L, OWN_P):
            gather.send(kind, k)

    def relay_near(gather, k):
        gather.arrived(FROM_LEFT, k)
        gather.send(FWD_R, k)
        gather.send(L_TO_P, k)
        gather.arrived(FROM_RIGHT, k)
        gather.send(FWD_L, k)
        gather.send(R_TO_P, k)

    def relay_far(gather, k):
        gather.arrived(FAR, k)
        gather.send(FAR_TO_P, k)

    tok_in.wait()
    pl.semaphore_wait(barrier, 3)
    for k in range(n_tchunk):
        send_own(Tokens, k)

    for b in range(n_seq):
        xg[b, me] = tok[b]

    phi_in.wait()
    lens_in.wait()
    g = gain[0]
    pn = unit(phi[...], 0).astype(BF16)
    pnt32 = pn.astype(F32).T
    for j in range(slabs):
        pnt[j] = pnt32[:, j * LANES:(j + 1) * LANES]

    def strided_rows(ref, start, size, stride):
        return jnp.concatenate([ref[j, pl.ds(start, size, stride=stride), :] for j in range(slabs)], axis=1)

    own_rows = jnp.concatenate([strided_rows(pnt, me * per_dev + s, n_exp, per_exp) for s in range(per_exp)], axis=0).astype(BF16)

    own = tok[...].reshape(own_tok, d_model)
    own_unit = unit(own, 1).astype(BF16)
    logits = g * jnp.dot(own_unit, pn, preferred_element_type=F32)
    comb = jnp.exp(logits - jnp.max(logits, axis=1, keepdims=True))
    rowinv[...] = 1.0 / jnp.sum(comb, axis=1, keepdims=True)
    comb = comb.astype(BF16)

    relay_near(Tokens, 0)

    width = 256
    devs = width // (CHUNK * rows)
    src = lax.broadcasted_iota(jnp.int32, (devs * per_dev, width), 0)
    col = lax.broadcasted_iota(jnp.int32, (devs * per_dev, width), 1)
    base = col // (CHUNK * rows) * per_dev + lax.rem(col, CHUNK * rows) // rows * per_exp + lax.rem(col, per_exp)
    row_seq = lax.broadcasted_iota(jnp.int32, (own_tok, width), 0) // n_tok
    col_seq = lax.rem(lax.broadcasted_iota(jnp.int32, (own_tok, width), 1), rows) // per_exp
    same = row_seq == col_seq

    def spread(k):
        pick = (src == base + k * (CHUNK * per_exp)).astype(F32).astype(BF16)
        for d in range(n_dev // devs):
            piece = jnp.dot(comb[:, d * devs * per_dev:(d + 1) * devs * per_dev], pick, preferred_element_type=F32)
            cexp[k, :, d * width:(d + 1) * width] = jnp.where(same, piece, 0.0).astype(BF16)

    share = n_chunk // (n_tchunk - 1)
    for t in range(1, n_tchunk):
        for k in range((t - 1) * share, n_chunk if t == n_tchunk - 1 else t * share):
            spread(k)
        relay_near(Tokens, t)

    pos = lax.broadcasted_iota(jnp.int32, (per_dev, all_tok), 1)

    def dispatch(b):
        x = xg[b].reshape(all_tok, d_model)
        xn = unit(x, 1).astype(BF16)
        lt = g * lax.dot_general(own_rows, xn, (((1,), (1,)), ((), ())), preferred_element_type=F32)
        lt = jnp.where(pos < lens[b], lt, NEG_FILL)
        e = jnp.exp(lt - jnp.max(lt, axis=1, keepdims=True))
        z = jnp.sum(e, axis=1, keepdims=True)
        s = jnp.dot(e.astype(BF16), x, preferred_element_type=F32) / z
        s = s.astype(BF16).astype(F32)
        for j in range(slabs):
            xs[j, b * per_dev:(b + 1) * per_dev, :] = s[:, j * LANES:(j + 1) * LANES]

    def dispatch_chunks(first, last):
        for k in range(first, last):
            Tokens.arrived(PARTNER, k)
        for b in range(first * SEQ_CHUNK, last * SEQ_CHUNK):
            dispatch(b)

    for k in range(n_tchunk):
        relay_far(Tokens, k)
    dispatch_chunks(0, n_tchunk // 2)
    dispatch_chunks(n_tchunk // 2, n_tchunk)

    def up(k, slot):
        for u in range(CHUNK):
            x = strided_rows(xs, k * CHUNK + u, rows, n_exp).astype(BF16)
            hid[u] = jax.nn.gelu(jnp.dot(x, w1[slot, u], preferred_element_type=F32)).astype(BF16)

    def down(k, slot):
        for u in range(CHUNK):
            yg[k, me, u] = jnp.dot(hid[u], w2[slot, u], preferred_element_type=F32).astype(BF16)

    w1_copy(0, 0).wait()
    up(0, 0)
    w1_copy(W_SLOTS, 0).start(priority=1)

    def step(k, carry):
        @pl.when(k >= 1)
        def _():
            send_own(Slots, k - 1)

        @pl.when(k >= LAG)
        def _():
            relay_near(Slots, k - LAG)

        slot, after = lax.rem(k, W_SLOTS), lax.rem(k + 1, W_SLOTS)
        w2_copy(k, slot).wait()
        w1_copy(k + 1, after).wait()
        down(k, slot)
        up(k + 1, after)

        @pl.when(k + W_SLOTS < n_chunk)
        def _():
            w2_copy(k + W_SLOTS, slot).start(priority=1)

        @pl.when(k + 1 + W_SLOTS < n_chunk)
        def _():
            w1_copy(k + 1 + W_SLOTS, after).start(priority=1)
        return carry

    lax.fori_loop(0, n_chunk - 1, step, 0)
    last = n_chunk - 1
    send_own(Slots, last - 1)
    w2_copy(last, last % W_SLOTS).wait()
    down(last, last % W_SLOTS)

    acc = jnp.zeros((own_tok, d_model), F32)

    def combine(acc, k):
        Slots.arrived(PARTNER, k)
        y = yg[k].reshape(n_dev * CHUNK * rows, d_model)
        return acc + jnp.dot(cexp[k], y, preferred_element_type=F32)

    first = last - LAG
    relay_near(Slots, first)
    send_own(Slots, last)
    far_done = comb_done = 0
    for k in range(first + 1, n_chunk):
        relay_near(Slots, k)
        for _ in range(2):
            if far_done < first - 1:
                relay_far(Slots, far_done)
                far_done += 1
                if far_done >= 3:
                    acc = combine(acc, comb_done)
                    comb_done += 1
    while far_done < n_chunk:
        relay_far(Slots, far_done)
        far_done += 1
        if far_done >= comb_done + 3:
            acc = combine(acc, comb_done)
            comb_done += 1
    while comb_done < n_chunk:
        acc = combine(acc, comb_done)
        comb_done += 1

    y = (acc * rowinv[...]).reshape(n_seq, n_tok, d_model)
    tpos = lax.broadcasted_iota(jnp.int32, (n_tok, d_model), 0) + me * n_tok
    for b in range(n_seq):
        out[b] = jnp.where(tpos < lens[b], y[b], 0.0).astype(BF16)

    Tokens.all_sent()
    Slots.all_sent()


def solution(mesh):
    n_dev = mesh.shape["seq"]

    def local_layer(tok_blk, len_blk, slot_param, logit_scale, w_in, w_out):
        n_seq, n_tok, d_model = tok_blk.shape
        n_exp, _, d_ff = w_in.shape
        n_slot = slot_param.shape[1]
        per_exp = n_slot // n_dev // n_exp
        rows = n_seq * per_exp
        n_chunk = n_exp // CHUNK
        vmem = pl.BlockSpec(memory_space=pltpu.VMEM)
        smem = pl.BlockSpec(memory_space=pltpu.SMEM)
        hbm = pl.BlockSpec(memory_space=pl.ANY)
        return pl.pallas_call(
            functools.partial(kernel, n_dev),
            out_shape=jax.ShapeDtypeStruct(tok_blk.shape, BF16),
            in_specs=[hbm, hbm, hbm, smem, hbm, hbm],
            out_specs=vmem,
            scratch_shapes=[
                pltpu.VMEM(tok_blk.shape, BF16),
                pltpu.VMEM(slot_param.shape, BF16),
                pltpu.SMEM(len_blk.shape, jnp.int32),
                pltpu.VMEM((n_seq, n_dev, n_tok, d_model), BF16),
                pltpu.VMEM((n_chunk, n_dev, CHUNK, rows, d_model), BF16),
                pltpu.VMEM((W_SLOTS, CHUNK, d_model, d_ff), BF16),
                pltpu.VMEM((W_SLOTS, CHUNK, d_ff, d_model), BF16),
                pltpu.VMEM((d_model // LANES, n_slot, LANES), F32),
                pltpu.VMEM((d_model // LANES, n_slot, LANES), F32),
                pltpu.VMEM((n_chunk, n_seq * n_tok, n_dev * CHUNK * rows), BF16),
                pltpu.VMEM((CHUNK, rows, d_ff), BF16),
                pltpu.VMEM((n_seq * n_tok, 1), F32),
                pltpu.SemaphoreType.DMA((3,)),
                pltpu.SemaphoreType.DMA((W_SLOTS,)),
                pltpu.SemaphoreType.DMA((W_SLOTS,)),
                pltpu.SemaphoreType.DMA,
                pltpu.SemaphoreType.DMA((4, n_seq // SEQ_CHUNK)),
                pltpu.SemaphoreType.DMA,
                pltpu.SemaphoreType.DMA((4, n_chunk)),
            ],
            compiler_params=pltpu.CompilerParams(collective_id=0, has_side_effects=True, vmem_limit_bytes=67000000),
            name="soft_moe",
        )(tok_blk, len_blk, slot_param, logit_scale.reshape(1), w_in, w_out)

    return jax.shard_map(local_layer, mesh=mesh, in_specs=(P("data", "seq", None), P("data"), P(None, None), P(), P("seq", None, None), P("seq", None, None)), out_specs=P("data", "seq", None), check_vma=False)
```

time: 165 us -> 41.6 us (0.25)
  waiting for transfers between devices: 85.3 us -> 0 us
  Pallas kernels: 0 us -> 39.2 us
  matrix products: 34 us -> 0 us
  blocking collectives: 24 us -> 0 us
  between operations: 13.9 us -> 0.66 us
  other arithmetic: 4.32 us -> 0 us
    pallas_call x0 -> x1, Pallas kernels: none -> 39.2 us  [local_layer(): pl.pallas_call(functools.partial(kernel, n_dev), out_shape=jax.ShapeDtype...]
    dot_general x4 -> x0, matrix products: 34 us -> none  [the longest x1 26.3 us: local_layer(): jnp.einsum('besf,efd->besd', hidden, w_out, preferred_element_type=jnp.fl...]
    reduce_scatter x1 -> x0, waiting for transfers between devices: 32.7 us -> none  [local_layer(): lax.psum_scatter(part_sum.astype(jnp.bfloat16), 'seq', scatter_dimension=...]
    all_gather x1 -> x0, waiting for transfers between devices: 26.9 us -> none  [local_layer(): lax.all_gather(own_out.reshape(batch_loc, slot_loc, d_model), 'seq', axis...]
    unnamed x4 -> x0, waiting for transfers between devices: 25.7 us -> none
    pmax x1 -> x0, blocking collectives: 24 us -> none  [local_layer(): col_max = lax.pmax(jnp.max(masked, axis=1, keepdims=True), 'seq')]
    reduce_sum x3 -> x0, other arithmetic: 2.43 us -> none  [the longest x2 2.15 us: l2_normed(): jnp.sum(v32 * v32, axis=axis_dim, keepdims=True) + EPSILON]
  transfers between devices with their start and end apart: 3 -> 0, of which waited for: 3 -> 0; matrix products, arithmetic and copies ran while one was open for 2% -> 0% of each run, Pallas kernels for 0% -> 0%
where the time goes in v2:
time: 41.6 us; the launch traced here: 41.5 us
  Pallas kernels  39.2 us (94%)
  local copies, waits for them, and re-layouts  1.62 us (4%)
  between operations  0.66 us (2%)
    pallas_call x1, Pallas kernels, local_layer(): pl.pallas_call(functools.partial(kernel, n_dev), out_shape=jax.ShapeDtype...  39.2 us
    unnamed x1, local copies, waits for them, and re-layouts  1.62 us

profile of v2, /device:TPU:81, one launch (start us, length us, event | category | flops | bytes accessed | tf_op | source)
XLA Modules:
  0.0 41.5 jit_solution(7131506416426871053)
XLA Ops:
  0.7 39.2 %soft_moe.1 = bf16[8,32,384]{2,1,0:T(8,128)(2,1)} custom-call(bf16[8,32,384]{2,1,0:T(8,128)(2,1)} %tok_hbm.1, s32[8]{0:T(128)} %lens_hbm.1, bf16[384,512]{1,0:T(8,128)(2,1)} %phi_hbm.1, f32[1]{0:T(128)} %bitcast.1.gain, bf16[32,384,1536]{2,1,0:T(8,128)(2,1)} %w_in.1, bf16[32,1536,384]{2,1,0:T(8,128)(2,1)} %w_out.1), custom_call_target="tpu_custom_call" | custom-call | tf_op jit(solution)/shard_map/soft_moe/pallas_call | solution.py:311
  39.9 1.6 %copy.9 = bf16[8,32,384]{2,1,0:T(8,128)(2,1)} copy(bf16[8,32,384]{2,1,0:T(8,128)(2,1)} %soft_moe.1) | data formatting | bytes 393216

commit v3 on v2

--- a/solution.py
+++ b/solution.py
@@ -14,15 +14,20 @@
 LANES = 128
 MESH = pl.DeviceIdType.MESH
 
-OWN_R, OWN_L, OWN_P, FWD_R, FWD_L, L_TO_P, R_TO_P, FAR_TO_P = range(8)
+OWN_R, OWN_L, OWN_P, FWD_R, FWD_L, FWD_R2, FWD_L2, L_TO_P, R_TO_P, FAR_TO_P = range(10)
 UNITS_SENT = 7
-UNITS_FROM_PARTNER = 4
-FROM_LEFT, FROM_RIGHT, FAR, PARTNER = range(4)
-RECV = {OWN_R: FROM_LEFT, OWN_L: FROM_RIGHT, FWD_R: FAR, FWD_L: FAR}
+FROM_LEFT, FROM_RIGHT, FAR, PARTNER, PARTNER_FAR = range(5)
+RECV = {OWN_R: FROM_LEFT, OWN_L: FROM_RIGHT, FWD_R: FAR, FWD_L: FAR, FWD_R2: PARTNER_FAR, FWD_L2: PARTNER_FAR, FAR_TO_P: PARTNER_FAR}
+UNITS = {PARTNER: 3}
+OWN, LEFT, RIGHT, ACROSS = 0, 2, 4, 6
+SRC_PLACE = {FWD_R: LEFT, FWD_L: RIGHT, FWD_R2: LEFT, FWD_L2: RIGHT, L_TO_P: LEFT, R_TO_P: RIGHT, FAR_TO_P: ACROSS}
+DST_PLACE = {OWN_R: LEFT, OWN_L: RIGHT, OWN_P: OWN + 1, FWD_R: ACROSS, FWD_L: ACROSS, FWD_R2: ACROSS + 1, FWD_L2: ACROSS + 1, L_TO_P: LEFT + 1, R_TO_P: RIGHT + 1, FAR_TO_P: ACROSS + 1}
 
 CHUNK = 4
 W_SLOTS = 5
 SEQ_CHUNK = 2
+TOK_BOTH = 3
+SLOT_BOTH = 7
 LAG = 4
 
 
@@ -32,7 +37,7 @@
 
 
 def kernel(n_dev, tok_hbm, lens_hbm, phi_hbm, gain, w_in, w_out, out,
-           tok, phi, lens, xg, yg, w1, w2, xs, pnt, cexp, hid, rowinv,
+           tok, phi, lens, xg, yg, w1, w2, xs, pnt, nlt, cexp, hid, rowinv,
            insem, sem1, sem2, tsend, trecv, ysend, yrecv):
     n_seq, n_tok, d_model = tok.shape
     n_exp = w_in.shape[0]
@@ -43,7 +48,6 @@
     n_chunk = n_exp // CHUNK
     n_tchunk = n_seq // SEQ_CHUNK
     n_chip = n_dev // 2
-    all_tok = n_dev * n_tok
     own_tok = n_seq * n_tok
     slabs = d_model // LANES
 
@@ -55,7 +59,8 @@
     partner = chip * 2 + 1 - core
 
     barrier = pltpu.get_barrier_semaphore()
-    for peer in (right, left, partner):
+    other = 1 - 2 * core
+    for peer in (right, left, right + other, left + other, partner):
         pl.semaphore_signal(barrier, inc=1, device_id={"seq": peer}, device_id_type=MESH)
 
     tok_in = pltpu.make_async_copy(tok_hbm, tok, insem.at[0])
@@ -75,13 +80,13 @@
         w1_copy(k, k).start(priority=1)
         w2_copy(k, k).start(priority=1)
 
-    dest = {OWN_R: right, OWN_L: left, FWD_R: right, FWD_L: left}
-    origins = {FWD_R: left, FWD_L: right, L_TO_P: left, R_TO_P: right, FAR_TO_P: far}
+    dest = {OWN_R: right, OWN_L: left, FWD_R: right, FWD_L: left, FWD_R2: right + other, FWD_L2: left + other}
+    origins = {FWD_R: left, FWD_L: right, FWD_R2: left, FWD_L2: right, L_TO_P: left, R_TO_P: right, FAR_TO_P: far}
 
     def part(kind, size):
-        if kind == FWD_R:
+        if kind in (FWD_R, FWD_R2):
             return 0, size // 2
-        if kind == FWD_L:
+        if kind in (FWD_L, FWD_L2):
             return size // 2, size // 2
         return 0, size
 
@@ -90,16 +95,17 @@
                                             device_id={"seq": device}, device_id_type=MESH)
 
     class Tokens:
+        both = TOK_BOTH
+
         def send(kind, k):
             lo, num = part(kind, SEQ_CHUNK)
             lo = lo + k * SEQ_CHUNK
-            dst = xg.at[pl.ds(lo, num), origins.get(kind, me)]
-            src = dst if kind in origins else tok.at[pl.ds(lo, num)]
+            dst = xg.at[pl.ds(lo, num), DST_PLACE[kind]]
+            src = xg.at[pl.ds(lo, num), SRC_PLACE[kind]] if kind in SRC_PLACE else tok.at[pl.ds(lo, num)]
             remote(src, dst, tsend, trecv.at[RECV.get(kind, PARTNER), k], dest.get(kind, partner)).start()
 
         def arrived(what, k):
-            units = UNITS_FROM_PARTNER if what == PARTNER else 1
-            ref = xg.at[pl.ds(k * SEQ_CHUNK, SEQ_CHUNK), pl.ds(0, units)]
+            ref = xg.at[pl.ds(k * SEQ_CHUNK, SEQ_CHUNK), pl.ds(0, UNITS.get(what, 1))]
             remote(ref, ref, tsend, trecv.at[what, k], partner).wait_recv()
 
         def all_sent():
@@ -107,14 +113,15 @@
             remote(ref, ref, tsend, trecv.at[0, 0], partner).wait_send()
 
     class Slots:
+        both = SLOT_BOTH
+
         def send(kind, k):
             lo, num = part(kind, CHUNK)
             ref = yg.at[k, origins.get(kind, me), pl.ds(lo, num)]
             remote(ref, ref, ysend, yrecv.at[RECV.get(kind, PARTNER), k], dest.get(kind, partner)).start()
 
         def arrived(what, k):
-            units = UNITS_FROM_PARTNER if what == PARTNER else 1
-            ref = yg.at[k, pl.ds(0, units)]
+            ref = yg.at[k, pl.ds(0, UNITS.get(what, 1))]
             remote(ref, ref, ysend, yrecv.at[what, k], partner).wait_recv()
 
         def all_sent():
@@ -126,24 +133,30 @@
             gather.send(kind, k)
 
     def relay_near(gather, k):
+        both = isinstance(k, int) and k >= gather.both
         gather.arrived(FROM_LEFT, k)
         gather.send(FWD_R, k)
+        if both:
+            gather.send(FWD_R2, k)
         gather.send(L_TO_P, k)
         gather.arrived(FROM_RIGHT, k)
         gather.send(FWD_L, k)
+        if both:
+            gather.send(FWD_L2, k)
         gather.send(R_TO_P, k)
 
     def relay_far(gather, k):
         gather.arrived(FAR, k)
-        gather.send(FAR_TO_P, k)
+        if k < gather.both:
+            gather.send(FAR_TO_P, k)
 
     tok_in.wait()
-    pl.semaphore_wait(barrier, 3)
+    pl.semaphore_wait(barrier, 5)
     for k in range(n_tchunk):
         send_own(Tokens, k)
 
     for b in range(n_seq):
-        xg[b, me] = tok[b]
+        xg[b, OWN] = tok[b]
 
     phi_in.wait()
     lens_in.wait()
@@ -188,30 +201,53 @@
             spread(k)
         relay_near(Tokens, t)
 
-    pos = lax.broadcasted_iota(jnp.int32, (per_dev, all_tok), 1)
-
-    def dispatch(b):
-        x = xg[b].reshape(all_tok, d_model)
+    near = ACROSS
+    places = (me, partner, left, left + other, right, right + other, far, far + other)
+
+    def positions(first, last):
+        lane = lax.broadcasted_iota(jnp.int32, (per_dev, (last - first) * n_tok), 1)
+        device = jnp.full(lane.shape, places[first], jnp.int32)
+        for r in range(first + 1, last):
+            device = jnp.where(lane // n_tok == r - first, places[r], device)
+        return device * n_tok + lax.rem(lane, n_tok)
+
+    def part_logits(x, pos, b):
         xn = unit(x, 1).astype(BF16)
         lt = g * lax.dot_general(own_rows, xn, (((1,), (1,)), ((), ())), preferred_element_type=F32)
-        lt = jnp.where(pos < lens[b], lt, NEG_FILL)
-        e = jnp.exp(lt - jnp.max(lt, axis=1, keepdims=True))
-        z = jnp.sum(e, axis=1, keepdims=True)
-        s = jnp.dot(e.astype(BF16), x, preferred_element_type=F32) / z
+        return jnp.where(pos < lens[b], lt, NEG_FILL)
+
+    near_pos, far_pos = positions(0, near), positions(near, n_dev)
+
+    def tokens_of(b, first, last):
+        return xg[b, first:last].reshape((last - first) * n_tok, d_model)
+
+    def near_logits(k):
+        Tokens.arrived(PARTNER, k)
+        for b in range(k * SEQ_CHUNK, (k + 1) * SEQ_CHUNK):
+            nlt[b] = part_logits(tokens_of(b, 0, near), near_pos, b)
+
+    def dispatch(b):
+        lt_n, x_f = nlt[b], tokens_of(b, near, n_dev)
+        lt_f = part_logits(x_f, far_pos, b)
+        top = jnp.maximum(jnp.max(lt_n, axis=1, keepdims=True), jnp.max(lt_f, axis=1, keepdims=True))
+        e_n, e_f = jnp.exp(lt_n - top), jnp.exp(lt_f - top)
+        z = jnp.sum(e_n, axis=1, keepdims=True) + jnp.sum(e_f, axis=1, keepdims=True)
+        s = jnp.dot(e_n.astype(BF16), tokens_of(b, 0, near), preferred_element_type=F32)
+        s = (s + jnp.dot(e_f.astype(BF16), x_f, preferred_element_type=F32)) / z
         s = s.astype(BF16).astype(F32)
         for j in range(slabs):
             xs[j, b * per_dev:(b + 1) * per_dev, :] = s[:, j * LANES:(j + 1) * LANES]
 
-    def dispatch_chunks(first, last):
-        for k in range(first, last):
-            Tokens.arrived(PARTNER, k)
-        for b in range(first * SEQ_CHUNK, last * SEQ_CHUNK):
-            dispatch(b)
-
     for k in range(n_tchunk):
-        relay_far(Tokens, k)
-    dispatch_chunks(0, n_tchunk // 2)
-    dispatch_chunks(n_tchunk // 2, n_tchunk)
+        near_logits(k)
+        if k == 1:
+            relay_far(Tokens, 0)
+        if k >= 1:
+            relay_far(Tokens, k)
+    for k in range(n_tchunk):
+        Tokens.arrived(PARTNER_FAR, k)
+    for b in range(n_seq):
+        dispatch(b)
 
     def up(k, slot):
         for u in range(CHUNK):
@@ -260,12 +296,13 @@
 
     def combine(acc, k):
         Slots.arrived(PARTNER, k)
+        Slots.arrived(PARTNER_FAR, k)
         y = yg[k].reshape(n_dev * CHUNK * rows, d_model)
         return acc + jnp.dot(cexp[k], y, preferred_element_type=F32)
 
     first = last - LAG
+    send_own(Slots, last)
     relay_near(Slots, first)
-    send_own(Slots, last)
     far_done = comb_done = 0
     for k in range(first + 1, n_chunk):
         relay_near(Slots, k)
@@ -323,6 +360,7 @@
                 pltpu.VMEM((W_SLOTS, CHUNK, d_ff, d_model), BF16),
                 pltpu.VMEM((d_model // LANES, n_slot, LANES), F32),
                 pltpu.VMEM((d_model // LANES, n_slot, LANES), F32),
+                pltpu.VMEM((n_seq, n_slot // n_dev, ACROSS * n_tok), F32),
                 pltpu.VMEM((n_chunk, n_seq * n_tok, n_dev * CHUNK * rows), BF16),
                 pltpu.VMEM((CHUNK, rows, d_ff), BF16),
                 pltpu.VMEM((n_seq * n_tok, 1), F32),
@@ -330,9 +368,9 @@
                 pltpu.SemaphoreType.DMA((W_SLOTS,)),
                 pltpu.SemaphoreType.DMA((W_SLOTS,)),
                 pltpu.SemaphoreType.DMA,
-                pltpu.SemaphoreType.DMA((4, n_seq // SEQ_CHUNK)),
+                pltpu.SemaphoreType.DMA((5, n_seq // SEQ_CHUNK)),
                 pltpu.SemaphoreType.DMA,
-                pltpu.SemaphoreType.DMA((4, n_chunk)),
+                pltpu.SemaphoreType.DMA((5, n_chunk)),
             ],
             compiler_params=pltpu.CompilerParams(collective_id=0, has_side_effects=True, vmem_limit_bytes=67000000),
             name="soft_moe",

time: 41.6 us -> 40.6 us (0.976)
  Pallas kernels: 39.2 us -> 38.2 us
    pallas_call x1, Pallas kernels: 39.2 us -> 38.2 us  [local_layer(): pl.pallas_call(functools.partial(kernel, n_dev), out_shape=jax.ShapeDtype...]
where the time goes in v3:
time: 40.6 us; the launch traced here: 40.5 us
  Pallas kernels  38.2 us (94%)
  local copies, waits for them, and re-layouts  1.62 us (4%)
  between operations  0.66 us (2%)
    pallas_call x1, Pallas kernels, local_layer(): pl.pallas_call(functools.partial(kernel, n_dev), out_shape=jax.ShapeDtype...  38.2 us
    unnamed x1, local copies, waits for them, and re-layouts  1.62 us

profile of v3, /device:TPU:81, one launch (start us, length us, event | category | flops | bytes accessed | tf_op | source)
XLA Modules:
  0.0 40.5 jit_solution(12026152842996021155)
XLA Ops:
  0.7 38.2 %soft_moe.1 = bf16[8,32,384]{2,1,0:T(8,128)(2,1)} custom-call(bf16[8,32,384]{2,1,0:T(8,128)(2,1)} %tok_hbm.1, s32[8]{0:T(128)} %lens_hbm.1, bf16[384,512]{1,0:T(8,128)(2,1)} %phi_hbm.1, f32[1]{0:T(128)} %bitcast.1.gain, bf16[32,384,1536]{2,1,0:T(8,128)(2,1)} %w_in.1, bf16[32,1536,384]{2,1,0:T(8,128)(2,1)} %w_out.1), custom_call_target="tpu_custom_call" | custom-call | tf_op jit(solution)/shard_map/soft_moe/pallas_call | solution.py:348
  38.9 1.6 %copy.9 = bf16[8,32,384]{2,1,0:T(8,128)(2,1)} copy(bf16[8,32,384]{2,1,0:T(8,128)(2,1)} %soft_moe.1) | data formatting | bytes 393216

commit v4 on v3

--- a/solution.py
+++ b/solution.py
@@ -26,8 +26,8 @@
 CHUNK = 4
 W_SLOTS = 5
 SEQ_CHUNK = 2
-TOK_BOTH = 3
-SLOT_BOTH = 7
+TOK_BOTH = 2
+SLOT_BOTH = 6
 LAG = 4
 
 
@@ -238,16 +238,20 @@
         for j in range(slabs):
             xs[j, b * per_dev:(b + 1) * per_dev, :] = s[:, j * LANES:(j + 1) * LANES]
 
+    def dispatch_chunks(first, last):
+        for k in range(first, last):
+            if k >= Tokens.both:
+                relay_far(Tokens, k)
+            Tokens.arrived(PARTNER_FAR, k)
+        for b in range(first * SEQ_CHUNK, last * SEQ_CHUNK):
+            dispatch(b)
+
     for k in range(n_tchunk):
         near_logits(k)
-        if k == 1:
-            relay_far(Tokens, 0)
-        if k >= 1:
-            relay_far(Tokens, k)
-    for k in range(n_tchunk):
-        Tokens.arrived(PARTNER_FAR, k)
-    for b in range(n_seq):
-        dispatch(b)
+        if 1 <= k <= Tokens.both:
+            relay_far(Tokens, k - 1)
+    dispatch_chunks(0, 2)
+    dispatch_chunks(2, n_tchunk)
 
     def up(k, slot):
         for u in range(CHUNK):

time: 40.6 us -> 39.8 us (0.980)
  Pallas kernels: 38.2 us -> 37.5 us
    pallas_call x1, Pallas kernels: 38.2 us -> 37.5 us  [local_layer(): pl.pallas_call(functools.partial(kernel, n_dev), out_shape=jax.ShapeDtype...]
where the time goes in v4:
time: 39.8 us; the launch traced here: 39.7 us
  Pallas kernels  37.5 us (94%)
  local copies, waits for them, and re-layouts  1.62 us (4%)
  between operations  0.66 us (2%)
    pallas_call x1, Pallas kernels, local_layer(): pl.pallas_call(functools.partial(kernel, n_dev), out_shape=jax.ShapeDtype...  37.5 us
    unnamed x1, local copies, waits for them, and re-layouts  1.62 us

profile of v4, /device:TPU:81, one launch (start us, length us, event | category | flops | bytes accessed | tf_op | source)
XLA Modules:
  0.0 39.7 jit_solution(96425046951944040)
XLA Ops:
  0.7 37.5 %soft_moe.1 = bf16[8,32,384]{2,1,0:T(8,128)(2,1)} custom-call(bf16[8,32,384]{2,1,0:T(8,128)(2,1)} %tok_hbm.1, s32[8]{0:T(128)} %lens_hbm.1, bf16[384,512]{1,0:T(8,128)(2,1)} %phi_hbm.1, f32[1]{0:T(128)} %bitcast.1.gain, bf16[32,384,1536]{2,1,0:T(8,128)(2,1)} %w_in.1, bf16[32,1536,384]{2,1,0:T(8,128)(2,1)} %w_out.1), custom_call_target="tpu_custom_call" | custom-call | tf_op jit(solution)/shard_map/soft_moe/pallas_call | solution.py:352
  38.1 1.6 %copy.9 = bf16[8,32,384]{2,1,0:T(8,128)(2,1)} copy(bf16[8,32,384]{2,1,0:T(8,128)(2,1)} %soft_moe.1) | data formatting | bytes 393216

commit v5 on v4

--- a/solution.py
+++ b/solution.py
@@ -253,8 +253,8 @@
     dispatch_chunks(0, 2)
     dispatch_chunks(2, n_tchunk)
 
-    def up(k, slot):
-        for u in range(CHUNK):
+    def up(k, slot, experts=range(CHUNK)):
+        for u in experts:
             x = strided_rows(xs, k * CHUNK + u, rows, n_exp).astype(BF16)
             hid[u] = jax.nn.gelu(jnp.dot(x, w1[slot, u], preferred_element_type=F32)).astype(BF16)
 
@@ -265,9 +265,17 @@
     w1_copy(0, 0).wait()
     up(0, 0)
     w1_copy(W_SLOTS, 0).start(priority=1)
+    w2_copy(0, 0).wait()
+    w1_copy(1, 1).wait()
+    down(0, 0)
+    up(1, 1, range(1))
+    send_own(Slots, 0)
+    up(1, 1, range(1, CHUNK))
+    w2_copy(W_SLOTS, 0).start(priority=1)
+    w1_copy(W_SLOTS + 1, 1).start(priority=1)
 
     def step(k, carry):
-        @pl.when(k >= 1)
+        @pl.when(k >= 2)
         def _():
             send_own(Slots, k - 1)
 
@@ -290,7 +298,7 @@
             w1_copy(k + 1 + W_SLOTS, after).start(priority=1)
         return carry
 
-    lax.fori_loop(0, n_chunk - 1, step, 0)
+    lax.fori_loop(1, n_chunk - 1, step, 0)
     last = n_chunk - 1
     send_own(Slots, last - 1)
     w2_copy(last, last % W_SLOTS).wait()

time: 39.8 us -> 40 us (level)
  no operation moved by 1% of the time
where the time goes in v5:
time: 40 us; the launch traced here: 39.9 us
  Pallas kernels  37.6 us (94%)
  local copies, waits for them, and re-layouts  1.62 us (4%)
  between operations  0.66 us (2%)
    pallas_call x1, Pallas kernels, local_layer(): pl.pallas_call(functools.partial(kernel, n_dev), out_shape=jax.ShapeDtype...  37.6 us
    unnamed x1, local copies, waits for them, and re-layouts  1.62 us

profile of v5, /device:TPU:81, one launch (start us, length us, event | category | flops | bytes accessed | tf_op | source)
XLA Modules:
  0.0 39.9 jit_solution(3347590953867874282)
XLA Ops:
  0.7 37.6 %soft_moe.1 = bf16[8,32,384]{2,1,0:T(8,128)(2,1)} custom-call(bf16[8,32,384]{2,1,0:T(8,128)(2,1)} %tok_hbm.1, s32[8]{0:T(128)} %lens_hbm.1, bf16[384,512]{1,0:T(8,128)(2,1)} %phi_hbm.1, f32[1]{0:T(128)} %bitcast.1.gain, bf16[32,384,1536]{2,1,0:T(8,128)(2,1)} %w_in.1, bf16[32,1536,384]{2,1,0:T(8,128)(2,1)} %w_out.1), custom_call_target="tpu_custom_call" | custom-call | tf_op jit(solution)/shard_map/soft_moe/pallas_call | solution.py:360
  38.2 1.6 %copy.9 = bf16[8,32,384]{2,1,0:T(8,128)(2,1)} copy(bf16[8,32,384]{2,1,0:T(8,128)(2,1)} %soft_moe.1) | data formatting | bytes 393216
